TPU v7x, 32 devices: a whole 2x2x4 slice. The times are simulated.
32 devices in a mesh: shard: 8 (over z, x), rep: 4 (over y, core).
Axes of the slice: x: 2, y: 2, z: 4, core: 2. Of those that a mesh axis runs over, the one named last changes fastest.
Arguments:
- activations: bfloat16 [4, 2048, 2048], P(None, ('shard', 'rep')), may hold values from -6 to 6
- value_grad: bfloat16 [4, 2048, 512], P(None, ('shard', 'rep')), may hold values from -6 to 6
- norm_gain: bfloat16 [2048], P('shard'), may hold values from 0.25 to 4.5
- value_weight: bfloat16 [2048, 512], P('shard'), may hold values from -0.125 to 0.125
Outputs:
- input_grad: bfloat16 [4, 2048, 2048], P(None, ('shard', 'rep'))
- weight_update: float32 [2048, 512], P('shard')
All inputs are finite; a program needn't handle non-finite values.
Results may differ from a plain program's by a relative error of at most 0.0029.
Values may be sent and summed in bfloat16 or wider, within the bound.
No kernel may reach another device: no remote copies, remote signals or barrier semaphores. Data moves between devices by JAX's collectives and lax.ppermute only.
A program may use at most 64 MiB of HBM per device.

v0:
```python
import jax
import jax.numpy as jnp
from jax import lax
from jax.sharding import PartitionSpec as P


def on_device(activations, value_grad, norm_gain, value_weight):
    gain_all, weight_all = (
        lax.all_gather(norm_gain, "shard", axis=0, tiled=True),
        lax.all_gather(value_weight, "shard", axis=0, tiled=True),
    )
    gain = gain_all.astype(jnp.float32)
    width = activations.shape[2]
    columns = value_grad.shape[2]

    def one_batch(total, inputs):
        block, cotangent = inputs
        values = block.astype(jnp.float32)
        rstd = lax.rsqrt(jnp.mean(values * values, axis=-1, keepdims=True) + 1e-05)
        normed = (values * rstd * gain).astype(jnp.bfloat16)
        total = total + lax.dot_general(
            normed, cotangent, (((0,), (0,)), ((), ())), preferred_element_type=jnp.float32
        )
        normed_grad = jnp.dot(cotangent, weight_all.T, preferred_element_type=jnp.float32)
        scaled = normed_grad * gain
        inner = jnp.mean(scaled * values, axis=-1, keepdims=True)
        result = (rstd * scaled - values * rstd * rstd * rstd * inner).astype(jnp.bfloat16)
        return (total, result)

    start = jnp.zeros((width, columns), jnp.float32)
    grad_full, input_grad = lax.scan(one_batch, start, (activations, value_grad))
    partial_rows = lax.psum_scatter(grad_full, "shard", scatter_dimension=0, tiled=True)
    summed = lax.psum(partial_rows, "rep")
    squares = lax.psum(jnp.sum(summed * summed), "shard")
    factor = 1.0 / jnp.maximum(1.0, jnp.sqrt(squares / (width * columns)))
    return (input_grad, summed * factor)


def solution(mesh):
    in_specs = (
        P(None, ("shard", "rep"), None),
        P(None, ("shard", "rep"), None),
        P("shard"),
        P("shard", None),
    )
    out_specs = (P(None, ("shard", "rep"), None), P("shard", None))
    return jax.shard_map(
        on_device, mesh=mesh, in_specs=in_specs, out_specs=out_specs, check_vma=False
    )
```

profile of v0, /device:TPU:0, one launch (start us, length us, event | category | flops | bytes accessed | tf_op | source)
XLA Modules:
  0.0 250.8 jit_solution(5175639290680449490)
XLA Ops:
  7.2 0.0 all-gather.3.cloned.1.call-start
  7.2 0.7 all-gather.3.cloned.1.call-update
  7.9 0.0 reduce-scatter.2.cloned.1.call-start
  8.0 0.7 reshape.34
  8.6 22.4 %all-gather = bf16[8,1,256]{2,1,0:T(2,128)(2,1)S(1)} all-gather(bf16[1,1,256]{2,1,0:T(2,128)(2,1)S(1)} %reshape.34), channel_id=1, replica_groups=mesh['shard'=8,'rep'=4] {'shard'}, dimensions={0}, use_global_device_ids=true | all-gather | bytes 4608 | tf_op jit(solution)/shard_map/all_gather | solution.py:9
  31.0 31.0 %all-gather.3.cloned.1.call-done = bf16[2048,512]{1,0:T(8,128)(2,1)} async-done(((bf16[256,512]{1,0:T(8,128)(2,1)}), bf16[2048,512]{1,0:T(8,128)(2,1)}) %all-gather.3.cloned.1.call-update) | async-done | bytes 2097168 | tf_op jit(solution)/shard_map/all_gather | solution.py:10
  62.0 33.5 %while.13 = (s32[]{:T(128)}, f32[2048,512]{1,0:T(8,128)}, bf16[4,64,2048]{2,1,0:T(8,128)(2,1)S(1)}, bf16[4,64,2048]{2,1,0:T(8,128)(2,1)}, f32[2048]{0:T(1024)S(1...) while((s32[]{:T(128)}, f32[2048,512]{1,0:T(8,128)}, ...), condition=%wide.region_3.4_spmd.clone, body=%wide.region_0.3_spmd.clone.sunk | while | flops 272891968 | bytes 12735858 | solution.py:31
  62.0 2.5 fusion.34
  64.5 1.2 fusion.35
  65.6 3.7 %select_add_fusion.2 = f32[2048,512]{1,0:T(8,128)} fusion(f32[2048,512]{1,0:T(8,128)} %get-tuple-element.148, pred[]{:T(512)S(6)} %compare.3, f32[2048]{0:T(1024)S(1)} %get-tuple-element.160, f32[64]{0:T(128)S(1)} %get-tuple-element.135, bf16[4,64,2048]{2,1,0:T(8,128)(2,1)} %get-tuple-element.159, s32[]{:T(128)S(6)} %copy.10, ...), kind=kOutput, calls=%fused_computation.clone.1 | convolution fusion | flops 136839168 | bytes 8726272 | tf_op jit(solution)/shard_map/while/body/eval_jaxpr/dot_general | solution.py:21
  69.3 2.5 fusion.34
  71.8 1.2 fusion.35
  73.0 5.1 %select_add_fusion.2 = f32[2048,512]{1,0:T(8,128)} fusion(f32[2048,512]{1,0:T(8,128)} %get-tuple-element.148, pred[]{:T(512)S(6)} %compare.3, f32[2048]{0:T(1024)S(1)} %get-tuple-element.160, f32[64]{0:T(128)S(1)} %get-tuple-element.135, bf16[4,64,2048]{2,1,0:T(8,128)(2,1)} %get-tuple-element.159, s32[]{:T(128)S(6)} %copy.10, ...), kind=kOutput, calls=%fused_computation.clone.1 | convolution fusion | flops 136839168 | bytes 8726272 | tf_op jit(solution)/shard_map/while/body/eval_jaxpr/dot_general | solution.py:21
  78.0 2.5 fusion.34
  80.5 1.2 fusion.35
  81.7 5.1 %select_add_fusion.2 = f32[2048,512]{1,0:T(8,128)} fusion(f32[2048,512]{1,0:T(8,128)} %get-tuple-element.148, pred[]{:T(512)S(6)} %compare.3, f32[2048]{0:T(1024)S(1)} %get-tuple-element.160, f32[64]{0:T(128)S(1)} %get-tuple-element.135, bf16[4,64,2048]{2,1,0:T(8,128)(2,1)} %get-tuple-element.159, s32[]{:T(128)S(6)} %copy.10, ...), kind=kOutput, calls=%fused_computation.clone.1 | convolution fusion | flops 136839168 | bytes 8726272 | tf_op jit(solution)/shard_map/while/body/eval_jaxpr/dot_general | solution.py:21
  86.7 2.5 fusion.34
  89.2 1.2 fusion.35
  90.4 5.1 %select_add_fusion.2 = f32[2048,512]{1,0:T(8,128)} fusion(f32[2048,512]{1,0:T(8,128)} %get-tuple-element.148, pred[]{:T(512)S(6)} %compare.3, f32[2048]{0:T(1024)S(1)} %get-tuple-element.160, f32[64]{0:T(128)S(1)} %get-tuple-element.135, bf16[4,64,2048]{2,1,0:T(8,128)(2,1)} %get-tuple-element.159, s32[]{:T(128)S(6)} %copy.10, ...), kind=kOutput, calls=%fused_computation.clone.1 | convolution fusion | flops 136839168 | bytes 8726272 | tf_op jit(solution)/shard_map/while/body/eval_jaxpr/dot_general | solution.py:21
  95.5 0.0 copy-start
  95.5 0.0 reduce-scatter.2.cloned.1.call-update
  95.5 0.0 all-reduce.2.cloned.1.call-start
  95.5 87.0 %reduce-scatter.2.cloned.1.call-done = f32[256,512]{1,0:T(8,128)} async-done(((f32[2048,512]{1,0:T(8,128)}), f32[256,512]{1,0:T(8,128)}) %reduce-scatter.2.cloned.1.call-update) | async-done | bytes 524304 | tf_op jit(solution)/shard_map/reduce_scatter | solution.py:32
  182.5 0.0 all-reduce.2.cloned.1.call-update
  182.5 35.4 %all-reduce.2.cloned.1.call-done = f32[256,512]{1,0:T(8,128)} async-done(((f32[256,512]{1,0:T(8,128)}), f32[256,512]{1,0:T(8,128)}) %all-reduce.2.cloned.1.call-update) | async-done | bytes 524304 | tf_op jit(solution)/shard_map/psum | solution.py:33
  217.9 1.8 multiply_reduce_fusion
  219.7 22.0 %psum.15 = f32[]{:T(128)} all-reduce(f32[]{:T(128)} %multiply_reduce_fusion), channel_id=1, replica_groups=mesh['shard'=8,'rep'=4] {'shard'}, use_global_device_ids=true, to_apply=%region_7.8 | all-reduce | flops 1 | bytes 8 | tf_op jit(solution)/shard_map/psum | solution.py:34
  242.4 1.9 broadcast_multiply_fusion.1
  244.3 0.0 copy-done
  (7 shorter events, 0.0 us)
Async XLA Ops:
  7.2 54.8 %all-gather.3.cloned.1.call-start = ((), (), s32[]{:S(2)}) async-start(), calls=%async_computation.1 | async-start | bytes 2359296 | tf_op jit(solution)/shard_map/all_gather | solution.py:10
  7.9 174.6 %reduce-scatter.2.cloned.1.call-start = ((), (), s32[]{:S(2)}) async-start(), calls=%async_computation.2 | async-start | bytes 4718592 | tf_op jit(solution)/shard_map/reduce_scatter | solution.py:32
  95.5 148.8 %copy-start = (bf16[4,64,2048]{2,1,0:T(8,128)(2,1)}, bf16[4,64,2048]{2,1,0:T(8,128)(2,1)S(1)}, u32[]{:S(2)}) copy-start(bf16[4,64,2048]{2,1,0:T(8,128)(2,1)S(1)} %get-tuple-element.38) | copy-start | bytes 3145732
  95.5 122.4 %all-reduce.2.cloned.1.call-start = ((), (), s32[]{:S(2)}) async-start(), calls=%async_computation.3 | async-start | bytes 1048576 | tf_op jit(solution)/shard_map/psum | solution.py:33
Sparse Core Ops, SparseCore 0:
  10.1 51.8 all-gather.2
  95.6 86.8 reduce-scatter.1
  184.8 33.0 all-reduce.1
where the time goes:
time: 251 us
  waiting for transfers between devices  154 us (61%)
  blocking collectives  44.3 us (18%)
  matrix products  28.8 us (11%)
  between operations  14.5 us (6%)
  other arithmetic  8.3 us (3%)
    reduce_scatter x1, waiting for transfers between devices, on_device(): lax.psum_scatter(grad_full, 'shard', scatter_dimension=0, tiled=True)  87 us
    psum x1, waiting for transfers between devices, on_device(): summed = lax.psum(partial_rows, 'rep')  35.4 us
    all_gather x1, waiting for transfers between devices, on_device(): lax.all_gather(value_weight, 'shard', axis=0, tiled=True)  31 us
    all_gather x1, blocking collectives, on_device(): lax.all_gather(norm_gain, 'shard', axis=0, tiled=True)  22.4 us
    psum x1, blocking collectives, on_device(): squares = lax.psum(jnp.sum(summed * summed), 'shard')  22 us
    dot_general x4, matrix products, one_batch(): lax.dot_general(normed, cotangent, (((0,), (0,)), ((), ())), preferred_el...  18.9 us
    dot_general x4, matrix products, one_batch(): jnp.dot(cotangent, weight_all.T, preferred_element_type=jnp.float32)  9.84 us
  transfers between devices with their start and end apart: 3, of which 3 were waited for; matrix products, arithmetic and copies ran while one was open for 0% of the time, Pallas kernels for 0%

commit v1 on v0

--- a/solution.py
+++ b/solution.py
@@ -30,7 +30,7 @@
     start = jnp.zeros((width, columns), jnp.float32)
     grad_full, input_grad = lax.scan(one_batch, start, (activations, value_grad))
     partial_rows = lax.psum_scatter(grad_full, "shard", scatter_dimension=0, tiled=True)
-    summed = lax.psum(partial_rows, "rep")
+    summed = jnp.sum(lax.all_gather(partial_rows, "rep"), axis=0)
     squares = lax.psum(jnp.sum(summed * summed), "shard")
     factor = 1.0 / jnp.maximum(1.0, jnp.sqrt(squares / (width * columns)))
     return (input_grad, summed * factor)

time: 251 us -> 239 us (0.952)
  waiting for transfers between devices: 154 us -> 142 us
    psum x1 -> x0, waiting for transfers between devices: 35.4 us -> none  [on_device(): summed = lax.psum(partial_rows, 'rep')]
    all_gather x0 -> x1, waiting for transfers between devices: none -> 23.8 us  [on_device(): summed = jnp.sum(lax.all_gather(partial_rows, 'rep'), axis=0)]
where the time goes in v1:
time: 239 us
  waiting for transfers between devices  142 us (59%)
  blocking collectives  44.3 us (19%)
  matrix products  28.8 us (12%)
  between operations  14.5 us (6%)
  other arithmetic  8.08 us (3%)
    reduce_scatter x1, waiting for transfers between devices, on_device(): lax.psum_scatter(grad_full, 'shard', scatter_dimension=0, tiled=True)  87 us
    all_gather x1, waiting for transfers between devices, on_device(): lax.all_gather(value_weight, 'shard', axis=0, tiled=True)  31 us
    all_gather x1, waiting for transfers between devices, on_device(): summed = jnp.sum(lax.all_gather(partial_rows, 'rep'), axis=0)  23.8 us
    all_gather x1, blocking collectives, on_device(): lax.all_gather(norm_gain, 'shard', axis=0, tiled=True)  22.4 us
    psum x1, blocking collectives, on_device(): squares = lax.psum(jnp.sum(summed * summed), 'shard')  22 us
    dot_general x4, matrix products, one_batch(): lax.dot_general(normed, cotangent, (((0,), (0,)), ((), ())), preferred_el...  18.9 us
    dot_general x4, matrix products, one_batch(): jnp.dot(cotangent, weight_all.T, preferred_element_type=jnp.float32)  9.84 us
  transfers between devices with their start and end apart: 3, of which 3 were waited for; matrix products, arithmetic and copies ran while one was open for 0% of the time, Pallas kernels for 0%

profile of v1, /device:TPU:0, one launch (start us, length us, event | category | flops | bytes accessed | tf_op | source)
XLA Modules:
  0.0 239.0 jit_solution(4784809478658846876)
XLA Ops:
  7.2 0.0 all-gather.5.cloned.1.call-start
  7.2 0.7 all-gather.5.cloned.1.call-update
  7.9 0.0 reduce-scatter.2.cloned.1.call-start
  8.0 0.7 reshape.35
  8.6 22.4 %all-gather.1 = bf16[8,1,256]{2,1,0:T(2,128)(2,1)S(1)} all-gather(bf16[1,1,256]{2,1,0:T(2,128)(2,1)S(1)} %reshape.35), channel_id=1, replica_groups=mesh['shard'=8,'rep'=4] {'shard'}, dimensions={0}, use_global_device_ids=true | all-gather | bytes 4608 | tf_op jit(solution)/shard_map/all_gather | solution.py:9
  31.0 31.0 %all-gather.5.cloned.1.call-done = bf16[2048,512]{1,0:T(8,128)(2,1)} async-done(((bf16[256,512]{1,0:T(8,128)(2,1)}), bf16[2048,512]{1,0:T(8,128)(2,1)}) %all-gather.5.cloned.1.call-update) | async-done | bytes 2097168 | tf_op jit(solution)/shard_map/all_gather | solution.py:10
  62.0 33.5 %while.13 = (s32[]{:T(128)}, f32[2048,512]{1,0:T(8,128)}, bf16[4,64,2048]{2,1,0:T(8,128)(2,1)S(1)}, bf16[4,64,2048]{2,1,0:T(8,128)(2,1)}, f32[2048]{0:T(1024)S(1...) while((s32[]{:T(128)}, f32[2048,512]{1,0:T(8,128)}, ...), condition=%wide.region_3.4_spmd.clone, body=%wide.region_0.3_spmd.clone.sunk | while | flops 272891968 | bytes 12735858 | solution.py:31
  62.0 2.5 %fusion.34 = (f32[64]{0:T(128)S(1)}, f32[64]{0:T(128)S(1)}, f32[64,2048]{1,0:T(8,128)S(1)}) fusion(bf16[4,64,2048]{2,1,0:T(8,128)(2,1)} %get-tuple-element.159, s32[]{:T(128)S(6)} %copy.10, f32[2048]{0:T(1024)S(1)} %get-tuple-element.160, bf16[2048,512]{1,0:T(8,128)(2,1)} %get-tuple-element.162, bf16[4,64,512]{2,1,0:T(8,128)(2,1)} %get-tuple-element.161), kind=kOutput, calls=%fused_computation.13.clone.1 | convolution fusion | flops 135004032 | bytes 2958848 | tf_op jit(solution)/shard_map/while/body/eval_jaxpr/dot_general | solution.py:24
  64.5 1.2 fusion.35
  65.6 3.7 %select_add_fusion.2 = f32[2048,512]{1,0:T(8,128)} fusion(f32[2048,512]{1,0:T(8,128)} %get-tuple-element.148, pred[]{:T(512)S(6)} %compare.3, f32[2048]{0:T(1024)S(1)} %get-tuple-element.160, f32[64]{0:T(128)S(1)} %get-tuple-element.135, bf16[4,64,2048]{2,1,0:T(8,128)(2,1)} %get-tuple-element.159, s32[]{:T(128)S(6)} %copy.10, ...), kind=kOutput, calls=%fused_computation.clone.1 | convolution fusion | flops 136839168 | bytes 8726272 | tf_op jit(solution)/shard_map/while/body/eval_jaxpr/dot_general | solution.py:21
  69.3 2.5 %fusion.34 = (f32[64]{0:T(128)S(1)}, f32[64]{0:T(128)S(1)}, f32[64,2048]{1,0:T(8,128)S(1)}) fusion(bf16[4,64,2048]{2,1,0:T(8,128)(2,1)} %get-tuple-element.159, s32[]{:T(128)S(6)} %copy.10, f32[2048]{0:T(1024)S(1)} %get-tuple-element.160, bf16[2048,512]{1,0:T(8,128)(2,1)} %get-tuple-element.162, bf16[4,64,512]{2,1,0:T(8,128)(2,1)} %get-tuple-element.161), kind=kOutput, calls=%fused_computation.13.clone.1 | convolution fusion | flops 135004032 | bytes 2958848 | tf_op jit(solution)/shard_map/while/body/eval_jaxpr/dot_general | solution.py:24
  71.8 1.2 fusion.35
  73.0 5.1 %select_add_fusion.2 = f32[2048,512]{1,0:T(8,128)} fusion(f32[2048,512]{1,0:T(8,128)} %get-tuple-element.148, pred[]{:T(512)S(6)} %compare.3, f32[2048]{0:T(1024)S(1)} %get-tuple-element.160, f32[64]{0:T(128)S(1)} %get-tuple-element.135, bf16[4,64,2048]{2,1,0:T(8,128)(2,1)} %get-tuple-element.159, s32[]{:T(128)S(6)} %copy.10, ...), kind=kOutput, calls=%fused_computation.clone.1 | convolution fusion | flops 136839168 | bytes 8726272 | tf_op jit(solution)/shard_map/while/body/eval_jaxpr/dot_general | solution.py:21
  78.0 2.5 %fusion.34 = (f32[64]{0:T(128)S(1)}, f32[64]{0:T(128)S(1)}, f32[64,2048]{1,0:T(8,128)S(1)}) fusion(bf16[4,64,2048]{2,1,0:T(8,128)(2,1)} %get-tuple-element.159, s32[]{:T(128)S(6)} %copy.10, f32[2048]{0:T(1024)S(1)} %get-tuple-element.160, bf16[2048,512]{1,0:T(8,128)(2,1)} %get-tuple-element.162, bf16[4,64,512]{2,1,0:T(8,128)(2,1)} %get-tuple-element.161), kind=kOutput, calls=%fused_computation.13.clone.1 | convolution fusion | flops 135004032 | bytes 2958848 | tf_op jit(solution)/shard_map/while/body/eval_jaxpr/dot_general | solution.py:24
  80.5 1.2 fusion.35
  81.7 5.1 %select_add_fusion.2 = f32[2048,512]{1,0:T(8,128)} fusion(f32[2048,512]{1,0:T(8,128)} %get-tuple-element.148, pred[]{:T(512)S(6)} %compare.3, f32[2048]{0:T(1024)S(1)} %get-tuple-element.160, f32[64]{0:T(128)S(1)} %get-tuple-element.135, bf16[4,64,2048]{2,1,0:T(8,128)(2,1)} %get-tuple-element.159, s32[]{:T(128)S(6)} %copy.10, ...), kind=kOutput, calls=%fused_computation.clone.1 | convolution fusion | flops 136839168 | bytes 8726272 | tf_op jit(solution)/shard_map/while/body/eval_jaxpr/dot_general | solution.py:21
  86.7 2.5 %fusion.34 = (f32[64]{0:T(128)S(1)}, f32[64]{0:T(128)S(1)}, f32[64,2048]{1,0:T(8,128)S(1)}) fusion(bf16[4,64,2048]{2,1,0:T(8,128)(2,1)} %get-tuple-element.159, s32[]{:T(128)S(6)} %copy.10, f32[2048]{0:T(1024)S(1)} %get-tuple-element.160, bf16[2048,512]{1,0:T(8,128)(2,1)} %get-tuple-element.162, bf16[4,64,512]{2,1,0:T(8,128)(2,1)} %get-tuple-element.161), kind=kOutput, calls=%fused_computation.13.clone.1 | convolution fusion | flops 135004032 | bytes 2958848 | tf_op jit(solution)/shard_map/while/body/eval_jaxpr/dot_general | solution.py:24
  89.2 1.2 fusion.35
  90.4 5.1 %select_add_fusion.2 = f32[2048,512]{1,0:T(8,128)} fusion(f32[2048,512]{1,0:T(8,128)} %get-tuple-element.148, pred[]{:T(512)S(6)} %compare.3, f32[2048]{0:T(1024)S(1)} %get-tuple-element.160, f32[64]{0:T(128)S(1)} %get-tuple-element.135, bf16[4,64,2048]{2,1,0:T(8,128)(2,1)} %get-tuple-element.159, s32[]{:T(128)S(6)} %copy.10, ...), kind=kOutput, calls=%fused_computation.clone.1 | convolution fusion | flops 136839168 | bytes 8726272 | tf_op jit(solution)/shard_map/while/body/eval_jaxpr/dot_general | solution.py:21
  95.5 0.0 copy-start
  95.5 0.0 reduce-scatter.2.cloned.1.call-update
  95.5 0.0 all-gather.7.cloned.1.call-start
  95.5 87.0 %reduce-scatter.2.cloned.1.call-done = f32[256,512]{1,0:T(8,128)} async-done(((f32[2048,512]{1,0:T(8,128)}), f32[256,512]{1,0:T(8,128)}) %reduce-scatter.2.cloned.1.call-update) | async-done | bytes 524304 | tf_op jit(solution)/shard_map/reduce_scatter | solution.py:32
  182.5 0.0 all-gather.7.cloned.1.call-update
  182.5 23.8 %all-gather.7.cloned.1.call-done = f32[1024,512]{1,0:T(8,128)} async-done(((f32[256,512]{1,0:T(8,128)}), f32[1024,512]{1,0:T(8,128)}) %all-gather.7.cloned.1.call-update) | async-done | bytes 2097168 | tf_op jit(solution)/shard_map/all_gather | solution.py:33
  206.3 1.9 reduce_sum.36
  208.2 0.7 multiply_reduce_fusion
  208.9 22.0 %psum.7 = f32[]{:T(128)} all-reduce(f32[]{:T(128)} %multiply_reduce_fusion), channel_id=1, replica_groups=mesh['shard'=8,'rep'=4] {'shard'}, use_global_device_ids=true, to_apply=%region_7.8 | all-reduce | flops 1 | bytes 8 | tf_op jit(solution)/shard_map/psum | solution.py:34
  231.6 0.8 broadcast_multiply_fusion.1
  232.4 0.0 copy-done
  (7 shorter events, 0.0 us)
Async XLA Ops:
  7.2 54.8 %all-gather.5.cloned.1.call-start = ((), (), s32[]{:S(2)}) async-start(), calls=%async_computation.1 | async-start | bytes 2359296 | tf_op jit(solution)/shard_map/all_gather | solution.py:10
  7.9 174.6 %reduce-scatter.2.cloned.1.call-start = ((), (), s32[]{:S(2)}) async-start(), calls=%async_computation.2 | async-start | bytes 4718592 | tf_op jit(solution)/shard_map/reduce_scatter | solution.py:32
  95.5 137.0 %copy-start = (bf16[4,64,2048]{2,1,0:T(8,128)(2,1)}, bf16[4,64,2048]{2,1,0:T(8,128)(2,1)S(1)}, u32[]{:S(2)}) copy-start(bf16[4,64,2048]{2,1,0:T(8,128)(2,1)S(1)} %get-tuple-element.38) | copy-start | bytes 3145732
  95.5 110.8 %all-gather.7.cloned.1.call-start = ((), (), s32[]{:S(2)}) async-start(), calls=%async_computation.3 | async-start | bytes 2621440 | tf_op jit(solution)/shard_map/all_gather | solution.py:33
Sparse Core Ops, SparseCore 0:
  10.1 51.8 all-gather.4
  95.6 86.8 reduce-scatter.1
  184.1 22.1 all-gather.6
